TPU v7x, 32 devices: a whole 2x2x4 slice. The times are simulated.
32 devices in a mesh: dp: 16 (over z, y, x), mp: 2 (over core).
Axes of the slice: x: 2, y: 2, z: 4, core: 2. Of those that a mesh axis runs over, the one named last changes fastest.
Arguments:
- pre_act: bfloat16 [8192, 16384], P('dp', 'mp'), may hold values from -8 to 8
- out_weight: bfloat16 [16384, 512], P('mp'), may hold values from -0.046875 to 0.046875
- out_grad: bfloat16 [8192, 512], P(('dp', 'mp')), may hold values from -2 to 2
Outputs:
- projected: bfloat16 [8192, 512], P(('dp', 'mp'))
- combined: float32 [16384, 512], P(('mp', 'dp'))
All inputs are finite; a program needn't handle non-finite values.
Results may differ from a plain program's by a relative error of at most 0.0005.
Values may be sent and summed in bfloat16 or wider, within the bound.
A program may use at most 128 MiB of HBM per device.

v0:
```python
import jax
import jax.numpy as jnp
from jax import lax
from jax.sharding import PartitionSpec as P

epsilon = 1e-06


def from_partner(value, axis, apart):
    mask = 2**apart
    pairs = [(source, source ^ mask) for source in range(lax.axis_size(axis))]
    return lax.ppermute(value, axis, pairs)


def contract(left, right):
    return lax.dot_general(
        left, right, (((0,), (0,)), ((), ())), preferred_element_type=jnp.float32
    )


def split_rows(piece, block, which):
    width = piece.shape[1]
    blocks = piece.reshape(piece.shape[0] // (2 * block), 2, block, width)
    kept = lax.dynamic_index_in_dim(blocks, which, 1, False).reshape(-1, width)
    sent = lax.dynamic_index_in_dim(blocks, 1 - which, 1, False).reshape(-1, width)
    return (kept, sent)


def partner_half(sent, level):
    return from_partner(sent, "dp", level)


def level_sums(partial_value, level):
    totals = lax.psum(partial_value, "mp")
    for inner_bit in range(level + 1):
        totals = totals + from_partner(totals, "dp", inner_bit)
    return totals


def merge_level(own, other, level, which):
    lower = which == 0
    own_sq = jnp.sum(own * own)
    other_sq = jnp.sum(other * other)
    partial_value = jnp.stack(
        [
            jnp.sum(own * other),
            jnp.where(lower, own_sq, other_sq),
            jnp.where(lower, other_sq, own_sq),
        ]
    )
    totals = level_sums(partial_value, level)
    first_coef = 1.0 - totals[0] / (2.0 * (totals[1] + epsilon))
    second_coef = 1.0 - totals[0] / (2.0 * (totals[2] + epsilon))
    own_coef = jnp.where(lower, first_coef, second_coef)
    other_coef = jnp.where(lower, second_coef, first_coef)
    return own_coef * own + other_coef * other


def local(pre_act, out_weight, out_grad):
    act = jnp.maximum(pre_act, jnp.zeros((), jnp.bfloat16))
    tokens = act.shape[0]
    partial_out = jnp.dot(act, out_weight, preferred_element_type=jnp.float32)
    summed = lax.psum_scatter(partial_out, "mp", scatter_dimension=0, tiled=True)
    projected = summed.astype(jnp.bfloat16)
    grad_full = lax.all_gather(out_grad, "mp", axis=0, tiled=True)
    count = lax.axis_size("dp")
    levels = count.bit_length() - 1
    me = lax.axis_index("dp")
    block = act.shape[1] // count
    first_bit = me & 1
    groups = act.reshape(tokens, act.shape[1] // (2 * block), 2, block)
    kept_act = lax.dynamic_index_in_dim(groups, first_bit, 2, False).reshape(tokens, -1)
    sent_act = lax.dynamic_index_in_dim(groups, 1 - first_bit, 2, False).reshape(tokens, -1)
    packed = jnp.concatenate([sent_act, grad_full], axis=1)
    arrived = from_partner(packed, "dp", 0)
    half = sent_act.shape[1]
    own = contract(kept_act, grad_full)
    other = contract(arrived[:, :half], arrived[:, half:])
    piece = merge_level(own, other, 0, first_bit)
    for level in range(1, levels):
        which = me >> level & 1
        own, sent = split_rows(piece, block, which)
        other = partner_half(sent, level)
        piece = merge_level(own, other, level, which)
    return (projected, piece)


def solution(mesh):
    placed = (P("dp", "mp"), P("mp", None), P(("dp", "mp"), None))
    return jax.shard_map(
        local,
        mesh=mesh,
        in_specs=placed,
        out_specs=(P(("dp", "mp"), None), P(("mp", "dp"), None)),
        check_vma=False,
    )
```

profile of v0, /device:TPU:0, one launch (start us, length us, event | category | flops | bytes accessed | tf_op | source)
XLA Modules:
  0.0 459.9 jit_solution(4458684051786192403)
XLA Ops:
  7.2 12.0 %copy.6 = bf16[512,8192]{0,1:T(8,128)(2,1)} copy(bf16[512,8192]{1,0:T(8,128)(2,1)} %param.3) | data formatting | bytes 16777216 | tf_op args[0]
  19.4 2.3 all_gather.3
  21.7 7.1 %broadcast_maximum_fusion = bf16[512,8192]{0,1:T(8,128)(2,1)} fusion(bf16[512,8192]{0,1:T(8,128)(2,1)} %copy.6), kind=kLoop, calls=%fused_computation.13 | loop fusion | flops 4194304 | bytes 16777216 | tf_op jit(solution)/shard_map/max | solution.py:60
  28.8 6.3 %constant_dynamic-slice_fusion.5 = (bf16[512,8,1,512]{0,3,2,1:T(8,128)(2,1)}, bf16[512,8,1,512]{0,3,2,1:T(8,128)(2,1)S(1)}) fusion(bf16[512,8,2,512]{0,3,2,1:T(8,128)(2,1)} %bitcast.58, s32[]{:T(128)S(6)} %select_n.77, s32[]{:T(128)S(6)} %select_n.78), kind=kLoop, calls=%fused_computation.34 | loop fusion | bytes 16777224 | tf_op jit(solution)/shard_map/jit(dynamic_index_in_dim)/dynamic_slice | solution.py:72
  35.1 2.5 pad_maximum_fusion
  37.5 2.8 collective-permute-start
  40.4 102.4 %collective-permute-done = bf16[512,4608]{0,1:T(8,128)(2,1)} collective-permute-done((bf16[512,4608]{0,1:T(8,128)(2,1)}, bf16[512,4608]{0,1:T(8,128)(2,1)}, u32[]{:S(2)}, u32[]{:S(2)}) %collective-permute-start) | collective-permute-done | bytes 4718624 | tf_op jit(solution)/shard_map/ppermute | solution.py:12
  142.8 4.7 %fusion = f32[4096,512]{1,0:T(8,128)S(1)} fusion(bf16[512,4608]{0,1:T(8,128)(2,1)} %collective-permute-done), kind=kOutput, calls=%fused_computation.5 | convolution fusion | flops 2147483648 | bytes 13107200 | tf_op jit(solution)/shard_map/dot_general | solution.py:16
  147.5 6.1 %multiply_reduce_fusion.2 = (f32[]{:T(128)}, f32[]{:T(128)}, f32[]{:T(128)}, f32[4096,512]{1,0:T(8,128)}) fusion(f32[4096,512]{1,0:T(8,128)S(1)} %fusion, bf16[512,4096]{0,1:T(8,128)(2,1)S(1)} %bitcast.59, bf16[512,512]{0,1:T(8,128)(2,1)S(1)} %all_gather.3), kind=kOutput, calls=%fused_computation.3 | convolution fusion | flops 2160066560 | bytes 21495820 | tf_op jit(solution)/shard_map/dot_general | solution.py:16
  156.8 2.4 psum.28
  166.0 11.1 %multiply_add_fusion = f32[4096,512]{1,0:T(8,128)} fusion(f32[4096,512]{1,0:T(8,128)} %copy-done, f32[4096,512]{1,0:T(8,128)} %get-tuple-element.32, f32[]{:T(128)S(6)} %select_n.82, f32[]{:T(128)S(6)} %select_n.81), kind=kLoop, calls=%fused_computation | loop fusion | flops 6291456 | bytes 25165832 | tf_op jit(solution)/shard_map/add | solution.py:56
  177.1 8.6 %multiply_reduce_fusion.4 = (f32[]{:T(128)}, f32[4,1,512,512]{3,2,1,0:T(8,128)}, f32[4,1,512,512]{3,2,1,0:T(8,128)}) fusion(f32[4,2,512,512]{3,2,1,0:T(8,128)} %bitcast.57, s32[]{:T(128)S(6)} %select_n.83, s32[]{:T(128)S(6)} %select_n.84), kind=kLoop, calls=%fused_computation.12 | loop fusion | flops 2097151 | bytes 16777228 | tf_op jit(solution)/shard_map/reduce_sum | solution.py:42
  187.5 90.1 %collective-permute-done.2 = f32[2048,512]{1,0:T(8,128)} collective-permute-done((f32[2048,512]{1,0:T(8,128)}, f32[2048,512]{1,0:T(8,128)}, u32[]{:S(2)}, u32[]{:S(2)}) %collective-permute-start.2) | collective-permute-done | bytes 4194336 | tf_op jit(solution)/shard_map/ppermute | solution.py:12
  277.6 5.1 %fusion.2 = (f32[]{:T(128)}, f32[]{:T(128)}) fusion(f32[2048,512]{1,0:T(8,128)} %collective-permute-done.2, f32[4,1,512,512]{3,2,1,0:T(8,128)} %get-tuple-element.15), kind=kLoop, calls=%fused_computation.9 | loop fusion | flops 4194302 | bytes 8388616 | tf_op jit(solution)/shard_map/reduce_sum | solution.py:46
  285.9 2.6 psum.29
  298.7 4.5 fusion.3
  303.2 2.4 multiply_reduce_fusion.6
  307.4 11.3 %fusion.10 = f32[512,512]{1,0:T(8,128)} fusion(bf16[8192,512]{1,0:T(8,128)(2,1)} %param.4, bf16[512,8192]{0,1:T(8,128)(2,1)} %copy.6), kind=kOutput, calls=%fused_computation.39 | convolution fusion | flops 4299161600 | bytes 17825792 | tf_op jit(solution)/shard_map/dot_general | solution.py:62
  318.7 32.7 %collective-permute-done.5 = f32[1024,512]{1,0:T(8,128)} collective-permute-done((f32[1024,512]{1,0:T(8,128)}, f32[1024,512]{1,0:T(8,128)}, u32[]{:S(2)}, u32[]{:S(2)}) %collective-permute-start.5) | collective-permute-done | bytes 2097184 | tf_op jit(solution)/shard_map/ppermute | solution.py:12
  351.4 2.8 fusion.4
  357.4 2.4 psum.30
  373.9 2.1 fusion.5
  377.4 2.8 collective-permute-start.9
  380.2 42.5 %collective-permute-done.9 = f32[512,512]{1,0:T(8,128)S(1)} collective-permute-done((f32[512,512]{1,0:T(8,128)S(1)}, f32[512,512]{1,0:T(8,128)S(1)}, u32[]{:S(2)}, u32[]{:S(2)}) %collective-permute-start.9) | collective-permute-done | bytes 1048608 | tf_op jit(solution)/shard_map/ppermute | solution.py:12
  422.7 2.2 fusion.6
  429.9 2.4 psum.31
  433.9 2.0 collective-permute-done.10
  437.5 2.0 collective-permute-done.11
  440.2 2.8 collective-permute-done.12
  443.1 2.1 collective-permute-start.13
  445.1 2.4 collective-permute-done.13
  450.7 2.4 fusion.8
  (49 shorter events, 37.6 us)
Async XLA Ops:
  7.2 420.9 %reduce-scatter.2.cloned.1.call-start = ((), (), s32[]{:S(2)}) async-start(), calls=%async_computation.1 | async-start | bytes 1572864 | tf_op jit(solution)/shard_map/reduce_scatter | solution.py:63
  7.2 12.0 %copy-start.3 = (bf16[256,512]{1,0:T(8,128)(2,1)S(1)}, bf16[256,512]{1,0:T(8,128)(2,1)}, u32[]{:S(2)}) copy-start(bf16[256,512]{1,0:T(8,128)(2,1)} %param.5) | copy-start | bytes 786436
  37.5 105.3 %collective-permute-start = (bf16[512,4608]{0,1:T(8,128)(2,1)}, bf16[512,4608]{0,1:T(8,128)(2,1)}, u32[]{:S(2)}, u32[]{:S(2)}) collective-permute-start(bf16[512,4608]{0,1:T(8,128)(2,1)} %pad_maximum_fusion), channel_id=1, source_target_pairs={{0,2},{2,0},{4,6},{6,4},{8,10},{10,8},{12,14},{14,12},{16,18},{18,... | collective-permute-start | bytes 14155784 | tf_op jit(solution)/shard_map/ppermute | solution.py:12
  40.4 107.1 %copy-start.1 = (bf16[512,8,1,512]{0,3,2,1:T(8,128)(2,1)S(1)}, bf16[512,8,1,512]{0,3,2,1:T(8,128)(2,1)}, u32[]{:S(2)}) copy-start(bf16[512,8,1,512]{0,3,2,1:T(8,128)(2,1)} %get-tuple-element.17) | copy-start | bytes 12582916
  147.5 6.1 %copy-start = (f32[4096,512]{1,0:T(8,128)}, f32[4096,512]{1,0:T(8,128)S(1)}, u32[]{:S(2)}) copy-start(f32[4096,512]{1,0:T(8,128)S(1)} %fusion) | copy-start | bytes 25165828
  159.3 3.6 collective-permute-start.1
  185.7 91.8 %collective-permute-start.2 = (f32[2048,512]{1,0:T(8,128)}, f32[2048,512]{1,0:T(8,128)}, u32[]{:S(2)}, u32[]{:S(2)}) collective-permute-start(f32[2048,512]{1,0:T(8,128)} %bitcast.10), channel_id=1, source_target_pairs={{0,4},{2,6},{4,0},{6,2},{8,12},{10,14},{12,8},{14,10},{16,20},{18,... | collective-permute-start | bytes 12582920 | tf_op jit(solution)/shard_map/ppermute | solution.py:12
  288.5 3.6 collective-permute-start.3
  292.1 3.6 collective-permute-start.4
  305.6 45.8 %collective-permute-start.5 = (f32[1024,512]{1,0:T(8,128)}, f32[1024,512]{1,0:T(8,128)}, u32[]{:S(2)}, u32[]{:S(2)}) collective-permute-start(f32[1024,512]{1,0:T(8,128)} %bitcast.18), channel_id=1, source_target_pairs={{0,8},{2,10},{4,12},{6,14},{8,0},{10,2},{12,4},{14,6},{16,24},{18,... | collective-permute-start | bytes 6291464 | tf_op jit(solution)/shard_map/ppermute | solution.py:12
  359.9 3.6 collective-permute-start.6
  363.4 3.6 collective-permute-start.7
  367.0 3.6 collective-permute-start.8
  375.9 1.4 copy-start.2
  377.4 45.3 %collective-permute-start.9 = (f32[512,512]{1,0:T(8,128)S(1)}, f32[512,512]{1,0:T(8,128)S(1)}, u32[]{:S(2)}, u32[]{:S(2)}) collective-permute-start(f32[512,512]{1,0:T(8,128)S(1)} %dynamic-slice_bitcast_fusion), channel_id=1, source_target_pairs={{0,16},{2,18},{4,20},{6,22},{8,24},{10,26},{12,28},{14,30},{16,0},... | collective-permute-start | bytes 3145736 | tf_op jit(solution)/shard_map/ppermute | solution.py:12
  432.3 3.6 collective-permute-start.10
  435.9 3.6 collective-permute-start.11
  439.5 3.6 collective-permute-start.12
  443.1 4.5 collective-permute-start.13
Sparse Core Ops, SparseCore 0:
  318.8 8.6 reduce-scatter.1
where the time goes:
time: 461 us; the launch traced here: 460 us
  waiting for transfers between devices  288 us (62%)
  other arithmetic  55.6 us (12%)
  between operations  34.2 us (7%)
  starting transfers between devices  25.5 us (6%)
  local copies, waits for them, and re-layouts  22.3 us (5%)
  matrix products  22 us (5%)
  blocking collectives  12.3 us (3%)
    ppermute x14, waiting for transfers between devices, from_partner(): return lax.ppermute(value, axis, pairs)  288 us
    ppermute x14, starting transfers between devices, from_partner(): return lax.ppermute(value, axis, pairs)  25.4 us
    add x4, other arithmetic, merge_level(): return own_coef * own + other_coef * other  20.1 us
    unnamed x10, local copies, waits for them, and re-layouts  13.5 us
    dot_general x1, matrix products, local(): partial_out = jnp.dot(act, out_weight, preferred_element_type=jnp.float32)  11.3 us
    reduce_sum x2, other arithmetic, merge_level(): own_sq = jnp.sum(own * own)  11 us
    dot_general x2, matrix products, contract(): lax.dot_general(left, right, (((0,), (0,)), ((), ())), preferred_element_...  10.8 us
    reduce_sum x3, other arithmetic, merge_level(): jnp.sum(own * other)  10.1 us
  transfers between devices with their start and end apart: 15, of which 14 were waited for; matrix products, arithmetic and copies ran while one was open for 4% of the time, Pallas kernels for 0%

commit v1 on v0

--- a/solution.py
+++ b/solution.py
@@ -1,9 +1,13 @@
+import functools
 import jax
 import jax.numpy as jnp
 from jax import lax
+from jax.experimental import pallas as pl
+from jax.experimental.pallas import tpu as pltpu
 from jax.sharding import PartitionSpec as P
 
 epsilon = 1e-06
+MESH = pl.DeviceIdType.MESH
 
 
 def from_partner(value, axis, apart):
@@ -24,10 +28,6 @@
     kept = lax.dynamic_index_in_dim(blocks, which, 1, False).reshape(-1, width)
     sent = lax.dynamic_index_in_dim(blocks, 1 - which, 1, False).reshape(-1, width)
     return (kept, sent)
-
-
-def partner_half(sent, level):
-    return from_partner(sent, "dp", level)
 
 
 def level_sums(partial_value, level):
@@ -56,7 +56,7 @@
     return own_coef * own + other_coef * other
 
 
-def local(pre_act, out_weight, out_grad):
+def halving(pre_act, out_weight, out_grad):
     act = jnp.maximum(pre_act, jnp.zeros((), jnp.bfloat16))
     tokens = act.shape[0]
     partial_out = jnp.dot(act, out_weight, preferred_element_type=jnp.float32)
@@ -80,9 +80,365 @@
     for level in range(1, levels):
         which = me >> level & 1
         own, sent = split_rows(piece, block, which)
-        other = partner_half(sent, level)
+        other = from_partner(sent, "dp", level)
         piece = merge_level(own, other, level, which)
     return (projected, piece)
+
+
+def put_lanes(values, rows):
+    padded = -(-len(values) // 8) * 8
+    strips = [jnp.sum(v, axis=0, keepdims=True) for v in values]
+    strips += [jnp.zeros_like(strips[0])] * (padded - len(values))
+    table = jnp.concatenate(strips, axis=0)
+    totals = jnp.sum(table, axis=1, keepdims=True)
+    lane = lax.broadcasted_iota(jnp.int32, table.shape, 1)
+    row = lax.broadcasted_iota(jnp.int32, table.shape, 0)
+    line = jnp.sum(jnp.where(lane == row, totals, 0.0), axis=0, keepdims=True)
+    return jnp.broadcast_to(line, (rows, line.shape[1]))
+
+
+def lane_value(line, p):
+    lane = lax.broadcasted_iota(jnp.int32, line.shape, 1)
+    return jnp.sum(jnp.where(lane == p, line, 0.0), axis=1, keepdims=True)
+
+
+def kernel(
+    n_dp, pre, w, og, proj, comb,
+    acts, grads_in, leaf, node, arrived, xbuf, wbuf, acc, part_in, slots, slots3,
+    act_send, act_recv, og_send, og_recv, mate_send, mate_recv, local_sem, own_sem,
+    fwd_sem, part_sem, slot_send, slot_recv, node_send, node_recv, slot3_send, slot3_recv,
+):
+    dp = lax.axis_index("dp")
+    core = lax.axis_index("mp")
+    group = n_dp // 2
+    bits = group.bit_length() - 1
+    me = lax.rem(dp, group)
+    high = dp // group
+    base = high * group
+    tokens = pre.shape[0]
+    block = pre.shape[1] // n_dp
+    own_rows = og.shape[0]
+    width = og.shape[1]
+    mate = 1 - core
+    me_bits = [lax.rem(me // 2**b, 2) for b in range(bits)]
+
+    def flip(r):
+        total = 0
+        for b in range(bits):
+            rb = (r // 2**b) % 2 if isinstance(r, int) else lax.rem(r // 2**b, 2)
+            total = total + 2**b * (me_bits[b] + rb - 2 * me_bits[b] * rb)
+        return total
+
+    barrier = pltpu.get_barrier_semaphore()
+    for q in range(1, 2 * n_dp):
+        other = lax.rem(dp * 2 + core + q, 2 * n_dp)
+        pl.semaphore_signal(
+            barrier, inc=1, device_id=(other // 2, lax.rem(other, 2)), device_id_type=MESH
+        )
+
+    my_og = grads_in.at[me, pl.ds(core * own_rows, own_rows)]
+    og_local = pltpu.make_async_copy(og, my_og, local_sem)
+    og_local.start()
+
+    def own_copy(h):
+        cols = pl.ds(pl.multiple_of((me + group * h) * block, block), block)
+        return pltpu.make_async_copy(pre.at[:, cols], acts.at[me, h], own_sem.at[h])
+
+    own_copy(0).start()
+    own_copy(1).start()
+    og_local.wait()
+    pl.semaphore_wait(barrier, 2 * n_dp - 1)
+
+    def og_copy(r, i, at):
+        rows = grads_in.at[at, pl.ds(core * own_rows, own_rows)]
+        return pltpu.make_async_remote_copy(
+            src_ref=rows, dst_ref=rows, send_sem=og_send.at[r], recv_sem=og_recv.at[r],
+            device_id=(base + i, core), device_id_type=MESH,
+        )
+
+    def act_copy(r, i, h, at):
+        cols = pl.ds(pl.multiple_of((i + group * h) * block, block), block)
+        return pltpu.make_async_remote_copy(
+            src_ref=pre.at[:, cols], dst_ref=acts.at[at, h],
+            send_sem=act_send.at[r, h], recv_sem=act_recv.at[r, h],
+            device_id=(base + i, core), device_id_type=MESH,
+        )
+
+    def mate_copy(r, i, side):
+        rows = grads_in.at[i, pl.ds(side * own_rows, own_rows)]
+        return pltpu.make_async_remote_copy(
+            src_ref=rows, dst_ref=rows, send_sem=mate_send.at[r], recv_sem=mate_recv.at[r],
+            device_id=(dp, mate), device_id_type=MESH,
+        )
+
+    mate_copy(0, me, core).start()
+    order = ORDER if group == 8 else list(range(1, group))
+    for r in order:
+        og_copy(r, flip(r), me).start()
+    for h in range(2):
+        for r in order:
+            act_copy(r, flip(r), h, me).start()
+
+    step_cols = xbuf.shape[2]
+    steps = pre.shape[1] // step_cols
+
+    def fetch(k, slot):
+        cols = pl.ds(pl.multiple_of(k * step_cols, step_cols), step_cols)
+        return (
+            pltpu.make_async_copy(pre.at[:, cols], xbuf.at[slot], fwd_sem.at[slot, 0]),
+            pltpu.make_async_copy(w.at[cols, :], wbuf.at[slot], fwd_sem.at[slot, 1]),
+        )
+
+    for c in fetch(0, 0):
+        c.start()
+    acc[...] = jnp.zeros_like(acc)
+
+    def forward(k, carry):
+        slot = lax.rem(k, 2)
+
+        @pl.when(k + 1 < steps)
+        def _():
+            for c in fetch(k + 1, 1 - slot):
+                c.start()
+
+        for c in fetch(k, slot):
+            c.wait()
+        x = jnp.maximum(xbuf[slot], jnp.zeros((), jnp.bfloat16))
+        acc[...] += jnp.dot(x, wbuf[slot], preferred_element_type=jnp.float32)
+        return carry
+
+    lax.fori_loop(0, steps, forward, 0)
+    part = pltpu.make_async_remote_copy(
+        src_ref=acc.at[pl.ds(mate * own_rows, own_rows)], dst_ref=part_in,
+        send_sem=part_sem.at[0], recv_sem=part_sem.at[1],
+        device_id=(dp, mate), device_id_type=MESH,
+    )
+    part.start()
+
+    for r in order:
+        i = flip(r)
+        og_copy(r, i, i).wait_recv()
+        mate_copy(r, i, core).start()
+    part.wait_recv()
+    proj[...] = (acc[pl.ds(core * own_rows, own_rows), :] + part_in[...]).astype(proj.dtype)
+    for r in range(group):
+        mate_copy(r, flip(r), mate).wait_recv()
+
+    pairs = [(i, j) for i in range(group) for j in range(i, group)]
+    sums = tuple(jnp.zeros((8, 128), jnp.float32) for _ in pairs)
+    for h in range(2):
+        def leaf_grad(i):
+            a = jnp.maximum(acts[i, h], jnp.zeros((), jnp.bfloat16))
+            leaf[i, pl.ds(h * block, block), :] = contract(a, grads_in[i])
+
+        own_copy(h).wait()
+        leaf_grad(me)
+        for r in order:
+            i = flip(r)
+            act_copy(r, i, h, i).wait_recv()
+            leaf_grad(i)
+
+        def gram(t, carry):
+            rows = pl.ds(pl.multiple_of(h * block + t * 8, 8), 8)
+            for c in range(width // 128):
+                v = [leaf[i, rows, c * 128:(c + 1) * 128] for i in range(group)]
+                carry = tuple(s + v[i] * v[j] for s, (i, j) in zip(carry, pairs))
+            return carry
+
+        sums = lax.fori_loop(0, block // 8, gram, sums)
+
+    mine = me * 2 + core
+    slots[mine] = put_lanes(list(sums), 8)
+
+    def slot_copy(q, other, at):
+        return pltpu.make_async_remote_copy(
+            src_ref=slots.at[at], dst_ref=slots.at[at],
+            send_sem=slot_send.at[q], recv_sem=slot_recv.at[at],
+            device_id=(base + other // 2, lax.rem(other, 2)), device_id_type=MESH,
+        )
+
+    for q in range(1, 2 * group):
+        slot_copy(q, lax.rem(mine + q, 2 * group), mine).start()
+    for q in range(1, 2 * group):
+        other = lax.rem(mine + q, 2 * group)
+        slot_copy(q, other, other).wait_recv()
+    line = slots[0]
+    for k in range(1, 2 * group):
+        line = line + slots[k]
+    line = line[0:1]
+    table = {}
+    for p, (i, j) in enumerate(pairs):
+        table[i, j] = table[j, i] = lane_value(line, p)
+    coef = [jnp.ones((1, 1), jnp.float32) for _ in range(group)]
+
+    def form(left, right):
+        total = jnp.zeros((1, 1), jnp.float32)
+        for i in left:
+            for j in right:
+                total = total + coef[i] * coef[j] * table[i, j]
+        return total
+
+    for level in range(bits):
+        size = 2**level
+        fresh = list(coef)
+        for start in range(0, group, 2 * size):
+            left = range(start, start + size)
+            right = range(start + size, start + 2 * size)
+            s = form(left, right)
+            first = 1.0 - s / (2.0 * (jnp.maximum(form(left, left), 0.0) + epsilon))
+            second = 1.0 - s / (2.0 * (jnp.maximum(form(right, right), 0.0) + epsilon))
+            for i in left:
+                fresh[i] = coef[i] * first
+            for j in right:
+                fresh[j] = coef[j] * second
+        coef = fresh
+
+    wide = [jnp.broadcast_to(c, (8, width)) for c in coef]
+
+    def build(h):
+        def strip(t, carry):
+            rows = pl.ds(pl.multiple_of(h * block + t * 8, 8), 8)
+            total = wide[0] * leaf[0, rows, :]
+            for i in range(1, group):
+                total = total + wide[i] * leaf[i, rows, :]
+            node[h, pl.ds(pl.multiple_of(t * 8, 8), 8), :] = total
+            return carry
+        lax.fori_loop(0, block // 8, strip, 0)
+
+    far = lax.rem(dp + group, n_dp)
+    pieces = node_send.shape[0]
+    tall = block // pieces
+
+    def node_copy(k):
+        rows = pl.ds(k * tall, tall)
+        return pltpu.make_async_remote_copy(
+            src_ref=node.at[1 - high, rows], dst_ref=arrived.at[rows],
+            send_sem=node_send.at[k], recv_sem=node_recv.at[k],
+            device_id=(far, core), device_id_type=MESH,
+        )
+
+    build(1 - high)
+    for k in range(pieces):
+        node_copy(k).start()
+    build(high)
+
+    sums = tuple(jnp.zeros((8, 128), jnp.float32) for _ in range(3))
+    for k in range(pieces):
+        node_copy(k).wait_recv()
+
+        def inner(t, carry):
+            rows = pl.ds(pl.multiple_of(k * tall + t * 8, 8), 8)
+            s, q, r = carry
+            for c in range(width // 128):
+                a = node[high, rows, c * 128:(c + 1) * 128]
+                b = arrived[rows, c * 128:(c + 1) * 128]
+                s, q, r = s + a * b, q + a * a, r + b * b
+            return s, q, r
+
+        sums = lax.fori_loop(0, tall // 8, inner, sums)
+    up = high.astype(jnp.float32)
+    low_sq = (1.0 - up) * sums[1] + up * sums[2]
+    high_sq = up * sums[1] + (1.0 - up) * sums[2]
+    place = dp * 2 + core
+    slots3[place] = put_lanes([sums[0], low_sq, high_sq], 8)
+
+    def slot3_copy(q, other, at):
+        return pltpu.make_async_remote_copy(
+            src_ref=slots3.at[at], dst_ref=slots3.at[at],
+            send_sem=slot3_send.at[q], recv_sem=slot3_recv.at[at],
+            device_id=(other // 2, lax.rem(other, 2)), device_id_type=MESH,
+        )
+
+    for q in range(1, 2 * n_dp):
+        slot3_copy(q, lax.rem(place + q, 2 * n_dp), place).start()
+    for q in range(1, 2 * n_dp):
+        other = lax.rem(place + q, 2 * n_dp)
+        slot3_copy(q, other, other).wait_recv()
+    line = slots3[0]
+    for k in range(1, 2 * n_dp):
+        line = line + slots3[k]
+    line = line[0:1]
+    s = lane_value(line, 0)
+    low = 1.0 - s / (2.0 * (lane_value(line, 1) + epsilon))
+    top = 1.0 - s / (2.0 * (lane_value(line, 2) + epsilon))
+    own_coef = jnp.broadcast_to((1.0 - up) * low + up * top, (8, width))
+    far_coef = jnp.broadcast_to(up * low + (1.0 - up) * top, (8, width))
+
+    def last(t, carry):
+        rows = pl.ds(pl.multiple_of(t * 8, 8), 8)
+        comb[rows, :] = own_coef * node[high, rows, :] + far_coef * arrived[rows, :]
+        return carry
+
+    lax.fori_loop(0, block // 8, last, 0)
+
+    mate_copy(0, me, core).wait_send()
+    for r in order:
+        i = flip(r)
+        og_copy(r, i, me).wait_send()
+        mate_copy(r, i, core).wait_send()
+        for h in range(2):
+            act_copy(r, i, h, me).wait_send()
+    part.wait_send()
+    for q in range(1, 2 * group):
+        slot_copy(q, lax.rem(mine + q, 2 * group), mine).wait_send()
+    for k in range(pieces):
+        node_copy(k).wait_send()
+    for q in range(1, 2 * n_dp):
+        slot3_copy(q, lax.rem(place + q, 2 * n_dp), place).wait_send()
+
+
+ORDER = [7, 3, 5, 6, 1, 2, 4]
+
+
+def exchange(n_dp, pre_act, out_weight, out_grad):
+    tokens, hidden = pre_act.shape
+    block = hidden // n_dp
+    group = n_dp // 2
+    width = out_grad.shape[1]
+    own_rows = out_grad.shape[0]
+    step_cols = hidden // 8
+    pieces = 4
+    dma = pltpu.SemaphoreType.DMA
+    hbm = pl.BlockSpec(memory_space=pl.ANY)
+    vmem = pl.BlockSpec(memory_space=pltpu.VMEM)
+    return pl.pallas_call(
+        functools.partial(kernel, n_dp),
+        out_shape=(
+            jax.ShapeDtypeStruct((own_rows, width), jnp.bfloat16),
+            jax.ShapeDtypeStruct((block, width), jnp.float32),
+        ),
+        in_specs=[hbm, hbm, hbm],
+        out_specs=(vmem, vmem),
+        scratch_shapes=[
+            pltpu.VMEM((group, 2, tokens, block), jnp.bfloat16),
+            pltpu.VMEM((group, tokens, width), jnp.bfloat16),
+            pltpu.VMEM((group, 2 * block, width), jnp.float32),
+            pltpu.VMEM((2, block, width), jnp.float32),
+            pltpu.VMEM((block, width), jnp.float32),
+            pltpu.VMEM((2, tokens, step_cols), jnp.bfloat16),
+            pltpu.VMEM((2, step_cols, width), jnp.bfloat16),
+            pltpu.VMEM((tokens, width), jnp.float32),
+            pltpu.VMEM((own_rows, width), jnp.float32),
+            pltpu.VMEM((2 * group, 8, 128), jnp.float32),
+            pltpu.VMEM((2 * n_dp, 8, 128), jnp.float32),
+            dma((group, 2)), dma((group, 2)), dma((group,)), dma((group,)),
+            dma((group,)), dma((group,)), dma, dma((2,)),
+            dma((2, 2)), dma((2,)), dma((2 * group,)), dma((2 * group,)),
+            dma((pieces,)), dma((pieces,)), dma((2 * n_dp,)), dma((2 * n_dp,)),
+        ],
+        compiler_params=pltpu.CompilerParams(
+            collective_id=0, has_side_effects=True, vmem_limit_bytes=60 * 2**20
+        ),
+    )(pre_act, out_weight, out_grad)
+
+
+def local(pre_act, out_weight, out_grad):
+    n_dp = lax.axis_size("dp")
+    block = pre_act.shape[1] // n_dp
+    rows = out_grad.shape[0]
+    if lax.axis_size("mp") == 2 and n_dp <= 16 and block % 128 == 0 and rows % 16 == 0:
+        return exchange(n_dp, pre_act, out_weight, out_grad)
+    return halving(pre_act, out_weight, out_grad)
 
 
 def solution(mesh):

time: 461 us -> 214 us (0.46)
  waiting for transfers between devices: 288 us -> 0 us
  Pallas kernels: 0 us -> 209 us
  other arithmetic: 55.6 us -> 0 us
  between operations: 34.2 us -> 0.64 us
  starting transfers between devices: 25.5 us -> 0 us
  matrix products: 22 us -> 0 us
  local copies, waits for them, and re-layouts: 22.3 us -> 3.93 us
  blocking collectives: 12.3 us -> 0 us
    ppermute x14 -> x0, waiting for transfers between devices: 288 us -> none  [from_partner(): return lax.ppermute(value, axis, pairs)]
    pallas_call x0 -> x1, Pallas kernels: none -> 209 us  [exchange(): pl.pallas_call(functools.partial(kernel, n_dp), out_shape=(jax.ShapeDtype...]
    ppermute x14 -> x0, starting transfers between devices: 25.4 us -> none  [from_partner(): return lax.ppermute(value, axis, pairs)]
    dot_general x3 -> x0, matrix products: 22 us -> none  [the longest x1 11.3 us: local(): partial_out = jnp.dot(act, out_weight, preferred_element_type=jnp.float32)]
    reduce_sum x5 -> x0, other arithmetic: 21.2 us -> none  [the longest x2 11 us: merge_level(): own_sq = jnp.sum(own * own)]
    add x14 -> x0, other arithmetic: 20.2 us -> none  [the longest x4 20.1 us: merge_level(): return own_coef * own + other_coef * other]
    psum x4 -> x0, blocking collectives: 9.96 us -> none  [level_sums(): totals = lax.psum(partial_value, 'mp')]
    unnamed x10 -> x2, local copies, waits for them, and re-layouts: 13.5 us -> 3.93 us
  transfers between devices with their start and end apart: 15 -> 0, of which waited for: 14 -> 0; matrix products, arithmetic and copies ran while one was open for 4% -> 0% of each run, Pallas kernels for 0% -> 0%
where the time goes in v1:
time: 214 us
  Pallas kernels  209 us (98%)
  local copies, waits for them, and re-layouts  3.93 us (2%)
    pallas_call x1, Pallas kernels, exchange(): pl.pallas_call(functools.partial(kernel, n_dp), out_shape=(jax.ShapeDtype...  209 us

profile of v1, /device:TPU:0, one launch (start us, length us, event | category | flops | bytes accessed | tf_op | source)
XLA Modules:
  0.0 213.9 jit_solution(16133819012140753694)
XLA Ops:
  0.6 209.3 %shard_map.50 = (bf16[256,512]{1,0:T(8,128)(2,1)}, f32[512,512]{1,0:T(8,128)}) custom-call(bf16[512,8192]{1,0:T(8,128)(2,1)} %pre.1, bf16[8192,512]{1,0:T(8,128)(2,1)} %w.1, bf16[256,512]{1,0:T(8,128)(2,1)} %og.1), custom_call_target="tpu_custom_call" | custom-call | tf_op jit(solution)/shard_map/pallas_call | solution.py:404
  209.9 1.7 copy.7
  211.6 2.3 %copy.8 = f32[512,512]{1,0:T(8,128)} copy(f32[512,512]{1,0:T(8,128)} %get-tuple-element.5) | data formatting | bytes 2097152

commit v2 on v1

--- a/solution.py
+++ b/solution.py
@@ -149,12 +149,21 @@
     og_local.wait()
     pl.semaphore_wait(barrier, 2 * n_dp - 1)
 
-    def og_copy(r, i, at):
+    def og_copy(r):
+        at, to = flip(RELAY[r][0]), flip(RELAY[r][1])
         rows = grads_in.at[at, pl.ds(core * own_rows, own_rows)]
         return pltpu.make_async_remote_copy(
             src_ref=rows, dst_ref=rows, send_sem=og_send.at[r], recv_sem=og_recv.at[r],
-            device_id=(base + i, core), device_id_type=MESH,
-        )
+            device_id=(base + to, core), device_id_type=MESH,
+        )
+
+    def og_arrival(r):
+        rows = grads_in.at[flip(r), pl.ds(core * own_rows, own_rows)]
+        pltpu.make_async_remote_copy(
+            src_ref=rows, dst_ref=rows, send_sem=og_send.at[r], recv_sem=og_recv.at[r],
+            device_id=(base + flip(r), core), device_id_type=MESH,
+        ).wait_recv()
+        mate_copy(r, flip(r), core).start()
 
     def act_copy(r, i, h, at):
         cols = pl.ds(pl.multiple_of((i + group * h) * block, block), block)
@@ -172,11 +181,21 @@
         )
 
     mate_copy(0, me, core).start()
-    order = ORDER if group == 8 else list(range(1, group))
-    for r in order:
-        og_copy(r, flip(r), me).start()
+    for r in (4, 1, 2):
+        og_copy(r).start()
+    act_copy(7, flip(7), 0, me).start()
+    og_arrival(2)
+    og_copy(6).start()
     for h in range(2):
-        for r in order:
+        for lead, _ in SLOTS:
+            if (lead, h) != (7, 0):
+                act_copy(lead, flip(lead), h, me).start()
+    og_arrival(4)
+    og_copy(5).start()
+    og_arrival(1)
+    og_copy(3).start()
+    for h in range(2):
+        for r in (2, 1, 3):
             act_copy(r, flip(r), h, me).start()
 
     step_cols = xbuf.shape[2]
@@ -215,10 +234,10 @@
     )
     part.start()
 
-    for r in order:
-        i = flip(r)
-        og_copy(r, i, i).wait_recv()
-        mate_copy(r, i, core).start()
+    og_arrival(6)
+    og_copy(7).start()
+    for r in (5, 3, 7):
+        og_arrival(r)
     part.wait_recv()
     proj[...] = (acc[pl.ds(core * own_rows, own_rows), :] + part_in[...]).astype(proj.dtype)
     for r in range(group):
@@ -226,18 +245,7 @@
 
     pairs = [(i, j) for i in range(group) for j in range(i, group)]
     sums = tuple(jnp.zeros((8, 128), jnp.float32) for _ in pairs)
-    for h in range(2):
-        def leaf_grad(i):
-            a = jnp.maximum(acts[i, h], jnp.zeros((), jnp.bfloat16))
-            leaf[i, pl.ds(h * block, block), :] = contract(a, grads_in[i])
-
-        own_copy(h).wait()
-        leaf_grad(me)
-        for r in order:
-            i = flip(r)
-            act_copy(r, i, h, i).wait_recv()
-            leaf_grad(i)
-
+    def gram_rows(h, sums):
         def gram(t, carry):
             rows = pl.ds(pl.multiple_of(h * block + t * 8, 8), 8)
             for c in range(width // 128):
@@ -245,7 +253,27 @@
                 carry = tuple(s + v[i] * v[j] for s, (i, j) in zip(carry, pairs))
             return carry
 
-        sums = lax.fori_loop(0, block // 8, gram, sums)
+        return lax.fori_loop(0, block // 8, gram, sums)
+
+    for h in range(2):
+        def leaf_grad(i):
+            a = jnp.maximum(acts[i, h], jnp.zeros((), jnp.bfloat16))
+            leaf[i, pl.ds(h * block, block), :] = contract(a, grads_in[i])
+
+        own_copy(h).wait()
+        leaf_grad(me)
+        for n, (lead, beside) in enumerate(SLOTS):
+            act_copy(lead, flip(lead), h, me).wait_send()
+            if h == 1 and n == 0:
+                sums = gram_rows(0, sums)
+            for r in (lead, beside):
+                if r:
+                    i = flip(r)
+                    act_copy(r, i, h, i).wait_recv()
+                    leaf_grad(i)
+
+        if h == 1:
+            sums = gram_rows(1, sums)
 
     mine = me * 2 + core
     slots[mine] = put_lanes(list(sums), 8)
@@ -372,12 +400,14 @@
     lax.fori_loop(0, block // 8, last, 0)
 
     mate_copy(0, me, core).wait_send()
-    for r in order:
+    for r in range(1, group):
         i = flip(r)
-        og_copy(r, i, me).wait_send()
+        og_copy(r).wait_send()
         mate_copy(r, i, core).wait_send()
-        for h in range(2):
-            act_copy(r, i, h, me).wait_send()
+    for _, r in SLOTS:
+        if r:
+            for h in range(2):
+                act_copy(r, flip(r), h, me).wait_send()
     part.wait_send()
     for q in range(1, 2 * group):
         slot_copy(q, lax.rem(mine + q, 2 * group), mine).wait_send()
@@ -387,7 +417,8 @@
         slot3_copy(q, lax.rem(place + q, 2 * n_dp), place).wait_send()
 
 
-ORDER = [7, 3, 5, 6, 1, 2, 4]
+SLOTS = ((7, 0), (5, 2), (6, 1), (4, 3))
+RELAY = {1: (0, 1), 2: (0, 2), 4: (0, 4), 3: (1, 2), 6: (2, 4), 5: (4, 1), 7: (6, 1)}
 
 
 def exchange(n_dp, pre_act, out_weight, out_grad):
@@ -436,7 +467,7 @@
     n_dp = lax.axis_size("dp")
     block = pre_act.shape[1] // n_dp
     rows = out_grad.shape[0]
-    if lax.axis_size("mp") == 2 and n_dp <= 16 and block % 128 == 0 and rows % 16 == 0:
+    if lax.axis_size("mp") == 2 and n_dp == 4 * len(SLOTS) and block % 128 == 0 and rows % 16 == 0:
         return exchange(n_dp, pre_act, out_weight, out_grad)
     return halving(pre_act, out_weight, out_grad)
 

time: 214 us -> 197 us (0.921)
  Pallas kernels: 209 us -> 192 us
    pallas_call x1, Pallas kernels: 209 us -> 192 us  [exchange(): pl.pallas_call(functools.partial(kernel, n_dp), out_shape=(jax.ShapeDtype...]
where the time goes in v2:
time: 197 us
  Pallas kernels  192 us (97%)
  local copies, waits for them, and re-layouts  3.93 us (2%)
    pallas_call x1, Pallas kernels, exchange(): pl.pallas_call(functools.partial(kernel, n_dp), out_shape=(jax.ShapeDtype...  192 us

profile of v2, /device:TPU:0, one launch (start us, length us, event | category | flops | bytes accessed | tf_op | source)
XLA Modules:
  0.0 196.5 jit_solution(13596292255640004105)
XLA Ops:
  0.6 191.9 %shard_map.50 = (bf16[256,512]{1,0:T(8,128)(2,1)}, f32[512,512]{1,0:T(8,128)}) custom-call(bf16[512,8192]{1,0:T(8,128)(2,1)} %pre.1, bf16[8192,512]{1,0:T(8,128)(2,1)} %w.1, bf16[256,512]{1,0:T(8,128)(2,1)} %og.1), custom_call_target="tpu_custom_call" | custom-call | tf_op jit(solution)/shard_map/pallas_call | solution.py:435
  192.6 1.7 copy.7
  194.2 2.3 %copy.8 = f32[512,512]{1,0:T(8,128)} copy(f32[512,512]{1,0:T(8,128)} %get-tuple-element.5) | data formatting | bytes 2097152
